TPU v7x, 32 devices: a whole 2x2x4 slice. The times are simulated.
32 devices in a mesh: sub: 8 (over z, x), fdr: 4 (over y, core).
Axes of the slice: x: 2, y: 2, z: 4, core: 2. Of those that a mesh axis runs over, the one named last changes fastest.
Arguments:
- inverse: bfloat16 [1024, 256, 256], P(('sub', 'fdr')), may hold values from -1 to 1
- cost: float32 [1024, 256, 128], P(('sub', 'fdr')), may hold values from -6 to 6
- lower_limit: float32 [1024, 256], P(('sub', 'fdr')), may hold values from -1.5 to -0.5
- upper_limit: float32 [1024, 256], P(('sub', 'fdr')), may hold values from 0.5 to 1.5
- iface_rows: int32 [1024, 6], P(('sub', 'fdr')), may hold values from 0 to 255, as said below
- substation_of: int32 [1024], P(('sub', 'fdr')), may hold values from 0 to 255, as said below
- live_count: int32 [32], P(('sub', 'fdr')), may hold values from 16 to 32
- reserve_weight: float32 [256], P('sub'), may hold values from 0.5 to 4
- reserve_target: float32 [256, 6, 128], P('sub'), may hold values from -6 to 6
Outputs:
- duals: float32 [1024, 6, 128], P(('sub', 'fdr'))
- consensus: float32 [256, 6, 128], P('sub')
- residual_norms: float32 [5, 2], replicated
- setpoints: float32 [1024, 256, 128], P(('sub', 'fdr'))
Inputs may be any that keep to these rules, and one draw needn't show every extreme that they name: `iface_rows`: each feeder's 6 interface rows are distinct. `substation_of`: of one device's 32 slots at most 6 hang from substations of one owner block (substations k * 32 to k * 32 + 31); for each index of fdr some block gets exactly 6 slots from every device with that index. `live_count`: a device's live feeders fill its first slots; the other slots hold unused data.
All inputs are finite; a program needn't handle non-finite values.
Results may differ from a plain program's by a relative error of at most 0.0069.
Values sent between devices are 32-bit elements; how exact they have to be, the bound alone decides.
No kernel may reach another device: no remote copies, remote signals or barrier semaphores. Data moves between devices by JAX's collectives and lax.ppermute only.
A program may use at most 128 MiB of HBM per device.

v0:
```python
import jax
import jax.numpy as jnp
from jax import lax
from jax.sharding import PartitionSpec as P

ITERS = 5
penalty = 2.0


def shards(
    inverse,
    cost,
    lower_limit,
    upper_limit,
    iface_rows,
    substation_of,
    live_count,
    reserve_weight,
    reserve_target,
):
    slot_count = inverse.shape[0]
    iface_count = iface_rows.shape[1]
    scenarios = cost.shape[2]
    flat_width = iface_count * scenarios
    sub_count = lax.axis_size("sub")
    owned_count = reserve_weight.shape[0]
    total_sub = owned_count * sub_count
    sub_index = lax.axis_index("sub")
    fdr_index = lax.axis_index("fdr")
    active = (jnp.arange(slot_count, dtype=jnp.int32) < live_count[0]).astype(jnp.float32)
    membership = (substation_of[:, None] == jnp.arange(total_sub, dtype=jnp.int32)[None, :]).astype(
        jnp.float32
    ) * active[:, None]
    tallied = lax.psum(jnp.sum(membership, axis=0), ("sub", "fdr"))
    flat_target = reserve_target.reshape(owned_count, flat_width)
    first_row = sub_index * owned_count
    dual_mask = (fdr_index == 0).astype(jnp.float32)
    overflow = max(1, slot_count // (2 * sub_count))
    capacity = max(2, slot_count // sub_count + overflow)
    slot_total = sub_count * capacity
    group_of = substation_of // owned_count
    group_hot = (group_of[:, None] == jnp.arange(sub_count, dtype=jnp.int32)[None, :]).astype(
        jnp.int32
    )
    earlier = jnp.cumsum(group_hot, axis=0) - group_hot
    slot_rank = jnp.sum(earlier * group_hot, axis=1)
    position = group_of * capacity + slot_rank
    slot_match = position[:, None] == jnp.arange(slot_total, dtype=jnp.int32)[None, :]
    slot_hot = slot_match.astype(jnp.float32)
    slot_ids = jnp.sum(slot_match.astype(jnp.int32) * (substation_of + 1)[:, None], axis=0) - 1
    arrived_ids = lax.all_to_all(slot_ids, "sub", split_axis=0, concat_axis=0, tiled=True)
    arrived_hot = (
        (arrived_ids - sub_index * owned_count)[:, None]
        == jnp.arange(owned_count, dtype=jnp.int32)[None, :]
    ).astype(jnp.float32)
    own_members = lax.dynamic_slice_in_dim(tallied, first_row, owned_count, 0)
    feeder_index = jnp.arange(slot_count, dtype=jnp.int32)[:, None]
    scaled_dual = jnp.zeros((slot_count, iface_count, scenarios), jnp.float32)
    local_consensus = jnp.zeros((slot_count, iface_count, scenarios), jnp.float32)
    anchor = jnp.zeros((slot_count, inverse.shape[1], scenarios), jnp.float32)
    old_rows = jnp.zeros((owned_count, flat_width), jnp.float32)
    sums_list = []
    for iteration in range(ITERS):
        right_side = (
            (anchor - cost)
            .at[feeder_index, iface_rows]
            .add(penalty * (local_consensus - scaled_dual))
            .astype(jnp.bfloat16)
        )
        primal = jnp.einsum("fkj,fjs->fks", inverse, right_side, preferred_element_type=jnp.float32)
        anchor = jnp.clip(primal, lower_limit[:, :, None], upper_limit[:, :, None])
        boundary = jnp.take_along_axis(primal, iface_rows[:, :, None], axis=1)
        outgoing = ((boundary + scaled_dual) * active[:, None, None]).reshape(
            slot_count, flat_width
        )
        packed = jnp.einsum("fn,fc->nc", slot_hot, outgoing, precision=lax.Precision.HIGHEST)
        arrived = lax.all_to_all(packed, "sub", split_axis=0, concat_axis=0, tiled=True)
        block_sums = jnp.einsum("no,nc->oc", arrived_hot, arrived, precision=lax.Precision.HIGHEST)
        collected = lax.psum(block_sums, "fdr")
        new_rows = (collected + reserve_weight[:, None] * flat_target) / (
            own_members + reserve_weight
        )[:, None]
        dual_local = dual_mask * jnp.sum(own_members[:, None] * (new_rows - old_rows) ** 2)
        old_rows = new_rows
        reply = jnp.einsum("no,oc->nc", arrived_hot, new_rows, precision=lax.Precision.HIGHEST)
        returned = lax.all_to_all(reply, "sub", split_axis=0, concat_axis=0, tiled=True)
        local_consensus = jnp.einsum(
            "fn,nc->fc", slot_hot, returned, precision=lax.Precision.HIGHEST
        ).reshape(slot_count, iface_count, scenarios)
        mismatch = boundary - local_consensus
        scaled_dual = (scaled_dual + mismatch) * active[:, None, None]
        primal_local = jnp.sum(active[:, None, None] * mismatch**2)
        primal_sum, dual_sum = lax.psum((primal_local, dual_local), ("sub", "fdr"))
        sums_list.append(jnp.stack([primal_sum, dual_sum]))
    stacked = jnp.stack(sums_list)
    residual_norms = jnp.sqrt(stacked) * jnp.array([1.0, penalty], jnp.float32)[None, :]
    consensus = old_rows.reshape(owned_count, iface_count, scenarios)
    return (penalty * scaled_dual, consensus, residual_norms, anchor * active[:, None, None])


def solution(mesh):
    placed = (
        P(("sub", "fdr"), None, None),
        P(("sub", "fdr"), None, None),
        P(("sub", "fdr"), None),
        P(("sub", "fdr"), None),
        P(("sub", "fdr"), None),
        P(("sub", "fdr")),
        P(("sub", "fdr")),
        P("sub"),
        P("sub", None, None),
    )
    return jax.shard_map(
        shards,
        mesh=mesh,
        in_specs=placed,
        out_specs=(
            P(("sub", "fdr"), None, None),
            P("sub", None, None),
            P(),
            P(("sub", "fdr"), None, None),
        ),
        check_vma=False,
    )
```

profile of v0, /device:TPU:0, one launch (start us, length us, event | category | flops | bytes accessed | tf_op | source)
XLA Modules:
  0.0 613.0 jit_solution(17046164565639930385)
XLA Ops:
  9.0 7.3 %all-to-all-start = ((s32[8,6,1]{1,2,0:T(1,128)}), s32[8,6,1]{1,2,0:T(1,128)S(1)}, u32[]{:S(2)}, u32[]{:S(2)}) async-start(s32[8,6,1]{1,2,0:T(1,128)} %bitcast.5), calls=%async_computation | async-start | bytes 8192 | tf_op jit(solution)/shard_map/all_to_all | solution.py:51
  17.7 5.6 copy.151
  23.3 4.6 broadcast_subtract_fusion
  29.0 20.0 %scatter_fusion = f32[32,256,128]{2,1,0:T(8,128)} fusion(f32[32,256,128]{2,1,0:T(8,128)} %broadcast_subtract_fusion, s32[192]{0:T(256)S(1)} %reshape.165, f32[192,128]{1,0:T(8,128)S(1)} %broadcast.263), kind=kCustom, calls=%fused_computation.5 | custom fusion | flops 24576 | bytes 296448 | tf_op jit(solution)/shard_map/scatter-add | solution.py:67
  49.1 9.3 %minimum_subtract_fusion.3 = (f32[32,256,128]{1,2,0:T(8,128)}, f32[32,256,128]{1,2,0:T(8,128)}) fusion(f32[32,256,128]{1,2,0:T(8,128)} %copy.151, f32[32,256]{1,0:T(8,128)S(1)} %copy-done.1, f32[32,256]{1,0:T(8,128)S(1)} %copy-done.2, bf16[32,256,256]{2,1,0:T(8,128)(2,1)} %param.12, f32[32,256,128]{2,1,0:T(8,128)} %scatter_fusion), kind=kOutput, calls=%fused_computation.14 | convolution fusion | flops 541065216 | bytes 21037056 | tf_op jit(solution)/shard_map/fkj,fjs->fks/dot_general | solution.py:70
  58.4 5.6 copy.144
  64.0 4.6 gather_fusion
  69.7 6.0 all-to-all-start.1
  75.9 40.7 %psum.113 = f32[256]{0:T(256)S(1)} all-reduce(f32[256]{0:T(256)S(1)} %select_reduce_fusion), channel_id=1, replica_groups=mesh['sub'=8,'fdr'=4] {'sub','fdr'}, use_global_device_ids=true, to_apply=%region_6.8 | all-reduce | flops 256 | bytes 2048 | tf_op jit(solution)/shard_map/psum | solution.py:34
  117.8 31.6 %all-reduce.7.cloned.1.call-done = f32[32,768]{1,0:T(8,128)} async-done(((f32[32,768]{1,0:T(8,128)}), f32[32,768]{1,0:T(8,128)}) %all-reduce.7.cloned.1.call-update) | async-done | bytes 98320 | tf_op jit(solution)/shard_map/psum | solution.py:79
  151.4 5.5 all-to-all-start.2
  156.9 5.6 copy.153
  162.5 2.2 all-to-all-done.2
  165.0 19.9 %scatter_fusion.1 = f32[32,256,128]{2,1,0:T(8,128)} fusion(f32[32,256,128]{2,1,0:T(8,128)} %copy.153, s32[192]{0:T(256)S(1)} %reshape.165, f32[192,128]{1,0:T(8,128)S(1)} %reshape.173), kind=kCustom, calls=%fused_computation.6 | custom fusion | flops 24576 | bytes 296448 | tf_op jit(solution)/shard_map/scatter-add | solution.py:67
  184.9 9.4 %minimum_subtract_fusion.2 = (f32[32,256,128]{1,2,0:T(8,128)}, f32[32,256,128]{1,2,0:T(8,128)}) fusion(f32[32,256,128]{1,2,0:T(8,128)} %copy.151, f32[32,256]{1,0:T(8,128)S(1)} %copy-done.1, f32[32,256]{1,0:T(8,128)S(1)} %copy-done.2, bf16[32,256,256]{2,1,0:T(8,128)(2,1)} %param.12, f32[32,256,128]{2,1,0:T(8,128)} %scatter_fusion.1), kind=kOutput, calls=%fused_computation.13 | convolution fusion | flops 541065216 | bytes 21037056 | tf_op jit(solution)/shard_map/fkj,fjs->fks/dot_general | solution.py:70
  194.3 5.6 copy.156
  199.8 4.6 gather_fusion.1
  204.9 11.5 %all_to_all.111 = f32[8,6,768]{2,1,0:T(8,128)S(1)} all-to-all(f32[8,6,768]{2,1,0:T(8,128)S(1)} %fusion.40), channel_id=1, replica_groups=mesh['sub'=8,'fdr'=4] {'sub'}, dimensions={0} | all-to-all | bytes 294912 | tf_op jit(solution)/shard_map/all_to_all | solution.py:77
  217.4 29.0 %all-reduce.9.cloned.1.call-done = f32[32,768]{1,0:T(8,128)} async-done(((f32[32,768]{1,0:T(8,128)}), f32[32,768]{1,0:T(8,128)}) %all-reduce.9.cloned.1.call-update) | async-done | bytes 98320 | tf_op jit(solution)/shard_map/psum | solution.py:79
  248.3 5.5 all-to-all-start.4
  253.9 5.6 copy.163
  262.0 19.9 %scatter_fusion.2 = f32[32,256,128]{2,1,0:T(8,128)} fusion(f32[32,256,128]{2,1,0:T(8,128)} %copy.163, s32[192]{0:T(256)S(1)} %reshape.165, f32[192,128]{1,0:T(8,128)S(1)} %reshape.179), kind=kCustom, calls=%fused_computation.7 | custom fusion | flops 24576 | bytes 296448 | tf_op jit(solution)/shard_map/scatter-add | solution.py:67
  281.8 9.4 %minimum_subtract_fusion.1 = (f32[32,256,128]{1,2,0:T(8,128)}, f32[32,256,128]{1,2,0:T(8,128)}) fusion(f32[32,256,128]{1,2,0:T(8,128)} %copy.151, f32[32,256]{1,0:T(8,128)S(1)} %copy-done.1, f32[32,256]{1,0:T(8,128)S(1)} %copy-done.2, bf16[32,256,256]{2,1,0:T(8,128)(2,1)} %param.12, f32[32,256,128]{2,1,0:T(8,128)} %scatter_fusion.2), kind=kOutput, calls=%fused_computation.12 | convolution fusion | flops 541065216 | bytes 21037056 | tf_op jit(solution)/shard_map/fkj,fjs->fks/dot_general | solution.py:70
  291.2 5.6 copy.166
  296.8 4.6 gather_fusion.2
  301.8 11.5 %all_to_all.112 = f32[8,6,768]{2,1,0:T(8,128)S(1)} all-to-all(f32[8,6,768]{2,1,0:T(8,128)S(1)} %fusion.38), channel_id=1, replica_groups=mesh['sub'=8,'fdr'=4] {'sub'}, dimensions={0} | all-to-all | bytes 294912 | tf_op jit(solution)/shard_map/all_to_all | solution.py:77
  314.3 28.9 %all-reduce.11.cloned.1.call-done = f32[32,768]{1,0:T(8,128)} async-done(((f32[32,768]{1,0:T(8,128)}), f32[32,768]{1,0:T(8,128)}) %all-reduce.11.cloned.1.call-update) | async-done | bytes 98320 | tf_op jit(solution)/shard_map/psum | solution.py:79
  345.2 5.5 all-to-all-start.6
  350.8 5.6 copy.173
  358.9 19.9 %scatter_fusion.3 = f32[32,256,128]{2,1,0:T(8,128)} fusion(f32[32,256,128]{2,1,0:T(8,128)} %copy.173, s32[192]{0:T(256)S(1)} %reshape.165, f32[192,128]{1,0:T(8,128)S(1)} %reshape.185), kind=kCustom, calls=%fused_computation.8 | custom fusion | flops 24576 | bytes 296448 | tf_op jit(solution)/shard_map/scatter-add | solution.py:67
  378.8 9.6 %minimum_subtract_fusion = (f32[32,256,128]{1,2,0:T(8,128)}, f32[32,256,128]{1,2,0:T(8,128)}) fusion(f32[32,256,128]{1,2,0:T(8,128)} %copy.151, f32[32,256]{1,0:T(8,128)S(1)} %copy-done.1, f32[32,256]{1,0:T(8,128)S(1)} %copy-done.2, bf16[32,256,256]{2,1,0:T(8,128)(2,1)} %param.12, f32[32,256,128]{2,1,0:T(8,128)} %scatter_fusion.3), kind=kOutput, calls=%fused_computation.11 | convolution fusion | flops 541065216 | bytes 21037056 | tf_op jit(solution)/shard_map/fkj,fjs->fks/dot_general | solution.py:70
  388.3 5.6 copy.176
  393.9 4.6 gather_fusion.3
  398.9 11.5 %all_to_all.113 = f32[8,6,768]{2,1,0:T(8,128)S(1)} all-to-all(f32[8,6,768]{2,1,0:T(8,128)S(1)} %fusion.36), channel_id=1, replica_groups=mesh['sub'=8,'fdr'=4] {'sub'}, dimensions={0} | all-to-all | bytes 294912 | tf_op jit(solution)/shard_map/all_to_all | solution.py:77
  411.4 28.9 %all-reduce.13.cloned.1.call-done = f32[32,768]{1,0:T(8,128)} async-done(((f32[32,768]{1,0:T(8,128)}), f32[32,768]{1,0:T(8,128)}) %all-reduce.13.cloned.1.call-update) | async-done | bytes 98320 | tf_op jit(solution)/shard_map/psum | solution.py:79
  442.3 5.5 all-to-all-start.8
  448.1 5.6 copy.183
  456.0 19.9 %scatter_fusion.4 = f32[32,256,128]{2,1,0:T(8,128)} fusion(f32[32,256,128]{2,1,0:T(8,128)} %copy.183, s32[192]{0:T(256)S(1)} %reshape.165, f32[192,128]{1,0:T(8,128)S(1)} %reshape.191), kind=kCustom, calls=%fused_computation.9 | custom fusion | flops 24576 | bytes 296448 | tf_op jit(solution)/shard_map/scatter-add | solution.py:67
  475.9 8.4 %minimum_multiply_fusion = (f32[32,256,128]{1,2,0:T(8,128)}, f32[32,256,128]{1,2,0:T(8,128)}) fusion(f32[32]{0:T(128)S(1)} %compare_convert_fusion, f32[32,256]{1,0:T(8,128)S(1)} %copy-done.1, f32[32,256]{1,0:T(8,128)S(1)} %copy-done.2, bf16[32,256,256]{2,1,0:T(8,128)(2,1)} %param.12, f32[32,256,128]{2,1,0:T(8,128)} %scatter_fusion.4), kind=kOutput, calls=%fused_computation.10 | convolution fusion | flops 541065216 | bytes 16842880 | tf_op jit(solution)/shard_map/fkj,fjs->fks/dot_general | solution.py:70
  484.2 5.6 copy.186
  489.8 4.6 gather_fusion.4
  494.8 11.5 %all_to_all.114 = f32[8,6,768]{2,1,0:T(8,128)S(1)} all-to-all(f32[8,6,768]{2,1,0:T(8,128)S(1)} %fusion.34), channel_id=1, replica_groups=mesh['sub'=8,'fdr'=4] {'sub'}, dimensions={0} | all-to-all | bytes 294912 | tf_op jit(solution)/shard_map/all_to_all | solution.py:77
  507.4 28.9 %all-reduce.15.cloned.1.call-done = f32[32,768]{1,0:T(8,128)} async-done(((f32[32,768]{1,0:T(8,128)}), f32[32,768]{1,0:T(8,128)}) %all-reduce.15.cloned.1.call-update) | async-done | bytes 98320 | tf_op jit(solution)/shard_map/psum | solution.py:79
  539.0 5.5 all-to-all-start.10
  544.5 5.6 copy.197
  555.6 43.2 %all-reduce = (f32[1]{0:T(128)}, f32[1]{0:T(128)}, f32[1]{0:T(128)}, f32[1]{0:T(128)}, f32[1]{0:T(128)}, /*index=5*/f32[1]{0:T(128)}, f32[1]{0:T(128)}, f32[1]{0:T(128)}, f32[1]{0:T(128)}, f32[1]{0:T(128)}) all-reduce(f32[1]{0:T(128)} %bitcast.21, f32[1]{0:T(128)} %bitcast.20, ...), channel_id=1, replica_groups=mesh['sub'=8,'fdr'=4] {'sub','fdr'}, use_global_device_ids=true, to_apply=%region_18.20 | all-reduce | flops 10 | bytes 80 | tf_op jit(solution)/shard_map/psum | solution.py:93
  598.7 2.6 maximum_bitcast_fusion
  603.0 2.5 maximum_bitcast_fusion.2
  (127 shorter events, 35.0 us)
Async XLA Ops:
  7.2 142.3 %copy-start = (f32[32,6,128]{2,0,1:T(8,128)S(1)}, f32[32,6,128]{2,0,1:T(8,128)}, u32[]{:S(2)}) copy-start(f32[32,6,128]{2,0,1:T(8,128)} %param.20) | copy-start | bytes 294916
  9.0 60.7 %all-to-all-start = ((s32[8,6,1]{1,2,0:T(1,128)}), s32[8,6,1]{1,2,0:T(1,128)S(1)}, u32[]{:S(2)}, u32[]{:S(2)}) async-start(s32[8,6,1]{1,2,0:T(1,128)} %bitcast.5), calls=%async_computation | async-start | bytes 8192 | tf_op jit(solution)/shard_map/all_to_all | solution.py:51
  23.3 25.8 %copy-start.1 = (f32[32,256]{1,0:T(8,128)S(1)}, f32[32,256]{1,0:T(8,128)}, u32[]{:S(2)}) copy-start(f32[32,256]{1,0:T(8,128)} %param.14) | copy-start | bytes 98308
  23.3 25.8 %copy-start.2 = (f32[32,256]{1,0:T(8,128)S(1)}, f32[32,256]{1,0:T(8,128)}, u32[]{:S(2)}) copy-start(f32[32,256]{1,0:T(8,128)} %param.15) | copy-start | bytes 98308
  58.4 17.4 %copy-start.5 = (s32[32]{0:T(128)S(1)}, s32[32]{0:T(128)}, u32[]{:S(2)}) copy-start(s32[32]{0:T(128)} %param.17) | copy-start | bytes 388
  58.4 59.3 %copy-start.3 = (f32[32]{0:T(128)S(1)}, f32[32]{0:T(128)}, u32[]{:S(2)}) copy-start(f32[32]{0:T(128)} %param.19) | copy-start | bytes 388
  69.7 47.0 %all-to-all-start.1 = ((f32[8,6,768]{2,1,0:T(8,128)}), f32[8,6,768]{2,1,0:T(8,128)S(1)}, u32[]{:S(2)}, u32[]{:S(2)}) async-start(f32[8,6,768]{2,1,0:T(8,128)} %fusion.42), calls=%async_computation.1 | async-start | bytes 393216 | tf_op jit(solution)/shard_map/all_to_all | solution.py:77
  75.7 73.7 %all-reduce.7.cloned.1.call-start = ((), (), s32[]{:S(2)}) async-start(), calls=%async_computation.11 | async-start | bytes 196608 | tf_op jit(solution)/shard_map/psum | solution.py:79
  151.4 13.3 %all-to-all-start.2 = ((f32[8,6,768]{2,1,0:T(8,128)}), f32[8,6,768]{2,1,0:T(8,128)S(1)}, u32[]{:S(2)}, u32[]{:S(2)}) async-start(f32[8,6,768]{2,1,0:T(8,128)} %all_to_all.77), calls=%async_computation.2 | async-start | bytes 393216 | tf_op jit(solution)/shard_map/all_to_all | solution.py:86
  156.9 89.5 %all-reduce.9.cloned.1.call-start = ((), (), s32[]{:S(2)}) async-start(), calls=%async_computation.12 | async-start | bytes 196608 | tf_op jit(solution)/shard_map/psum | solution.py:79
  248.3 13.3 %all-to-all-start.4 = ((f32[8,6,768]{2,1,0:T(8,128)}), f32[8,6,768]{2,1,0:T(8,128)S(1)}, u32[]{:S(2)}, u32[]{:S(2)}) async-start(f32[8,6,768]{2,1,0:T(8,128)} %all_to_all.82), calls=%async_computation.4 | async-start | bytes 393216 | tf_op jit(solution)/shard_map/all_to_all | solution.py:86
  253.8 89.5 %all-reduce.11.cloned.1.call-start = ((), (), s32[]{:S(2)}) async-start(), calls=%async_computation.13 | async-start | bytes 196608 | tf_op jit(solution)/shard_map/psum | solution.py:79
  345.2 13.3 %all-to-all-start.6 = ((f32[8,6,768]{2,1,0:T(8,128)}), f32[8,6,768]{2,1,0:T(8,128)S(1)}, u32[]{:S(2)}, u32[]{:S(2)}) async-start(f32[8,6,768]{2,1,0:T(8,128)} %all_to_all.87), calls=%async_computation.6 | async-start | bytes 393216 | tf_op jit(solution)/shard_map/all_to_all | solution.py:86
  350.7 89.7 %all-reduce.13.cloned.1.call-start = ((), (), s32[]{:S(2)}) async-start(), calls=%async_computation.14 | async-start | bytes 196608 | tf_op jit(solution)/shard_map/psum | solution.py:79
  442.3 13.3 %all-to-all-start.8 = ((f32[8,6,768]{2,1,0:T(8,128)}), f32[8,6,768]{2,1,0:T(8,128)S(1)}, u32[]{:S(2)}, u32[]{:S(2)}) async-start(f32[8,6,768]{2,1,0:T(8,128)} %all_to_all.92), calls=%async_computation.8 | async-start | bytes 393216 | tf_op jit(solution)/shard_map/all_to_all | solution.py:86
  447.8 88.5 %all-reduce.15.cloned.1.call-start = ((), (), s32[]{:S(2)}) async-start(), calls=%async_computation.15 | async-start | bytes 196608 | tf_op jit(solution)/shard_map/psum | solution.py:79
  539.0 15.0 %all-to-all-start.10 = ((f32[8,6,768]{2,1,0:T(8,128)}), f32[8,6,768]{2,1,0:T(8,128)S(1)}, u32[]{:S(2)}, u32[]{:S(2)}) async-start(f32[8,6,768]{2,1,0:T(8,128)} %all_to_all.97), calls=%async_computation.10 | async-start | bytes 393216 | tf_op jit(solution)/shard_map/all_to_all | solution.py:86
  544.5 61.3 %copy-start.4 = (f32[2]{0:T(128)S(1)}, f32[2]{0:T(128)}, u32[]{:S(2)}) copy-start(f32[2]{0:T(128)} %constant.68.clone) | copy-start | bytes 28
Sparse Core Ops, SparseCore 0:
  117.8 31.5 all-reduce.6
  217.5 28.7 all-reduce.8
  314.4 28.7 all-reduce.10
  411.6 28.7 all-reduce.12
  507.5 28.7 all-reduce.14
where the time goes:
time: 617 us; the launch traced here: 613 us
  waiting for transfers between devices  156 us (25%)
  blocking collectives  130 us (21%)
  other arithmetic  120 us (19%)
  local copies, waits for them, and re-layouts  91.1 us (15%)
  matrix products  56.4 us (9%)
  starting transfers between devices  41.3 us (7%)
  between operations  18.1 us (3%)
    psum x5, waiting for transfers between devices, shards(): collected = lax.psum(block_sums, 'fdr')  147 us
    scatter-add x5, other arithmetic, shards(): right_side = (anchor - cost).at[feeder_index, iface_rows].add(penalty * (...  99.5 us
    all_to_all x4, blocking collectives, shards(): lax.all_to_all(packed, 'sub', split_axis=0, concat_axis=0, tiled=True)  46.1 us
    dot_general x5, matrix products, shards(): jnp.einsum('fkj,fjs->fks', inverse, right_side, preferred_element_type=jn...  46 us
    psum x1, blocking collectives, shards(): primal_sum, dual_sum = lax.psum((primal_local, dual_local), ('sub', 'fdr'))  43.2 us
    psum x1, blocking collectives, shards(): tallied = lax.psum(jnp.sum(membership, axis=0), ('sub', 'fdr'))  40.7 us
    dot_general x5, local copies, waits for them, and re-layouts, shards(): jnp.einsum('fkj,fjs->fks', inverse, right_side, preferred_element_type=jn...  27.9 us
    all_to_all x5, starting transfers between devices, shards(): lax.all_to_all(reply, 'sub', split_axis=0, concat_axis=0, tiled=True)  27.6 us
  transfers between devices with their start and end apart: 12, of which 9 were waited for; matrix products, arithmetic and copies ran while one was open for 13% of the time, Pallas kernels for 0%

commit v1 on v0

--- a/solution.py
+++ b/solution.py
@@ -76,7 +76,16 @@
         packed = jnp.einsum("fn,fc->nc", slot_hot, outgoing, precision=lax.Precision.HIGHEST)
         arrived = lax.all_to_all(packed, "sub", split_axis=0, concat_axis=0, tiled=True)
         block_sums = jnp.einsum("no,nc->oc", arrived_hot, arrived, precision=lax.Precision.HIGHEST)
-        collected = lax.psum(block_sums, "fdr")
+
+        def extend_entries(local_block):
+            mesh_ax = "fdr"
+            q_n = lax.axis_size(mesh_ax)
+            main = local_block
+            for ii in [[(b, b ^ s) for b in range(q_n)] for s in (1, 2, 4, 8, 16) if s < q_n]:
+                main = main + lax.ppermute(main, mesh_ax, perm=ii)
+            return main
+
+        collected = extend_entries(block_sums)
         new_rows = (collected + reserve_weight[:, None] * flat_target) / (
             own_members + reserve_weight
         )[:, None]

time: 617 us -> 475 us (0.77)
  waiting for transfers between devices: 156 us -> 39.7 us
  between operations: 18.1 us -> 5.09 us
    psum x5 -> x0, waiting for transfers between devices: 147 us -> none  [shards(): collected = lax.psum(block_sums, 'fdr')]
    ppermute x0 -> x10, waiting for transfers between devices: none -> 23.6 us  [extend_entries(): main = main + lax.ppermute(main, mesh_ax, perm=ii)]
    all_to_all x5, starting transfers between devices: 27.6 us -> 18.2 us  [shards(): lax.all_to_all(reply, 'sub', split_axis=0, concat_axis=0, tiled=True)]
    all_to_all x1, waiting for transfers between devices: 0.01 us -> 7.68 us  [shards(): lax.all_to_all(packed, 'sub', split_axis=0, concat_axis=0, tiled=True)]
    ppermute x0 -> x10, starting transfers between devices: none -> 6.4 us  [extend_entries(): main = main + lax.ppermute(main, mesh_ax, perm=ii)]
  transfers between devices with their start and end apart: 12 -> 17, of which waited for: 9 -> 14; matrix products, arithmetic and copies ran while one was open for 13% -> 17% of each run, Pallas kernels for 0% -> 0%
where the time goes in v1:
time: 475 us; the launch traced here: 471 us
  blocking collectives  128 us (27%)
  other arithmetic  116 us (24%)
  local copies, waits for them, and re-layouts  91.1 us (19%)
  matrix products  53.2 us (11%)
  waiting for transfers between devices  39.7 us (8%)
  starting transfers between devices  37.9 us (8%)
  between operations  5.09 us (1%)
    scatter-add x5, other arithmetic, shards(): right_side = (anchor - cost).at[feeder_index, iface_rows].add(penalty * (...  99.5 us
    all_to_all x4, blocking collectives, shards(): lax.all_to_all(packed, 'sub', split_axis=0, concat_axis=0, tiled=True)  46.1 us
    dot_general x5, matrix products, shards(): jnp.einsum('fkj,fjs->fks', inverse, right_side, preferred_element_type=jn...  46 us
    psum x1, blocking collectives, shards(): primal_sum, dual_sum = lax.psum((primal_local, dual_local), ('sub', 'fdr'))  43.3 us
    psum x1, blocking collectives, shards(): tallied = lax.psum(jnp.sum(membership, axis=0), ('sub', 'fdr'))  38.6 us
    dot_general x5, local copies, waits for them, and re-layouts, shards(): jnp.einsum('fkj,fjs->fks', inverse, right_side, preferred_element_type=jn...  27.9 us
    ppermute x10, waiting for transfers between devices, extend_entries(): main = main + lax.ppermute(main, mesh_ax, perm=ii)  23.6 us
    gather x12, local copies, waits for them, and re-layouts, shards(): boundary = jnp.take_along_axis(primal, iface_rows[:, :, None], axis=1)  23 us
  transfers between devices with their start and end apart: 17, of which 14 were waited for; matrix products, arithmetic and copies ran while one was open for 17% of the time, Pallas kernels for 0%

profile of v1, /device:TPU:0, one launch (start us, length us, event | category | flops | bytes accessed | tf_op | source)
XLA Modules:
  0.0 470.7 jit_solution(7262412601604034130)
XLA Ops:
  2.5 7.3 %all-to-all-start = ((s32[8,6,1]{1,2,0:T(1,128)}), s32[8,6,1]{1,2,0:T(1,128)S(1)}, u32[]{:S(2)}, u32[]{:S(2)}) async-start(s32[8,6,1]{1,2,0:T(1,128)} %bitcast.5), calls=%async_computation | async-start | bytes 8192 | tf_op jit(solution)/shard_map/all_to_all | solution.py:51
  11.1 5.6 %copy.151 = f32[32,256,128]{1,2,0:T(8,128)} copy(f32[32,256,128]{2,1,0:T(8,128)} %param.13) | data formatting | bytes 8388608 | tf_op args[1]
  16.7 4.6 broadcast_subtract_fusion
  22.5 20.0 %scatter_fusion = f32[32,256,128]{2,1,0:T(8,128)} fusion(f32[32,256,128]{2,1,0:T(8,128)} %broadcast_subtract_fusion, s32[192]{0:T(256)S(1)} %reshape.165, f32[192,128]{1,0:T(8,128)S(1)} %broadcast.263), kind=kCustom, calls=%fused_computation.5 | custom fusion | flops 24576 | bytes 296448 | tf_op jit(solution)/shard_map/scatter-add | solution.py:67
  42.5 9.3 %minimum_subtract_fusion.3 = (f32[32,256,128]{1,2,0:T(8,128)}, f32[32,256,128]{1,2,0:T(8,128)}) fusion(f32[32,256,128]{1,2,0:T(8,128)} %copy.151, f32[32,256]{1,0:T(8,128)S(1)} %copy-done.1, f32[32,256]{1,0:T(8,128)S(1)} %copy-done.2, bf16[32,256,256]{2,1,0:T(8,128)(2,1)} %param.12, f32[32,256,128]{2,1,0:T(8,128)} %scatter_fusion), kind=kOutput, calls=%fused_computation.14 | convolution fusion | flops 541065216 | bytes 21037056 | tf_op jit(solution)/shard_map/fkj,fjs->fks/dot_general | solution.py:70
  51.9 5.6 %copy.144 = f32[32,256,128]{2,1,0:T(8,128)} copy(f32[32,256,128]{1,2,0:T(8,128)} %get-tuple-element.61) | data formatting | bytes 8388608 | tf_op jit(solution)/shard_map/fkj,fjs->fks/dot_general | solution.py:70
  57.5 4.6 gather_fusion
  63.2 6.0 %all-to-all-start.1 = ((f32[8,6,768]{2,1,0:T(8,128)}), f32[8,6,768]{2,1,0:T(8,128)S(1)}, u32[]{:S(2)}, u32[]{:S(2)}) async-start(f32[8,6,768]{2,1,0:T(8,128)} %fusion.42), calls=%async_computation.1 | async-start | bytes 393216 | tf_op jit(solution)/shard_map/all_to_all | solution.py:77
  69.3 7.7 %all-to-all-done.1 = f32[8,6,768]{2,1,0:T(8,128)S(1)} async-done(((f32[8,6,768]{2,1,0:T(8,128)}), f32[8,6,768]{2,1,0:T(8,128)S(1)}, u32[]{:S(2)}, u32[]{:S(2)}) %all-to-all-start.1) | async-done | bytes 147488 | tf_op jit(solution)/shard_map/all_to_all | solution.py:77
  77.5 38.6 %psum.77 = f32[256]{0:T(256)S(1)} all-reduce(f32[256]{0:T(256)S(1)} %select_reduce_fusion), channel_id=1, replica_groups=mesh['sub'=8,'fdr'=4] {'sub','fdr'}, use_global_device_ids=true, to_apply=%region_5.7 | all-reduce | flops 256 | bytes 2048 | tf_op jit(solution)/shard_map/psum | solution.py:34
  118.5 2.5 collective-permute-done.1
  122.1 4.4 all-to-all-start.2
  126.5 5.6 %copy.153 = f32[32,256,128]{2,1,0:T(8,128)} copy(f32[32,256,128]{1,2,0:T(8,128)} %get-tuple-element.60) | data formatting | bytes 8388608 | tf_op jit(solution)/shard_map/sub | solution.py:65
  134.7 19.9 %scatter_fusion.1 = f32[32,256,128]{2,1,0:T(8,128)} fusion(f32[32,256,128]{2,1,0:T(8,128)} %copy.153, s32[192]{0:T(256)S(1)} %reshape.165, f32[192,128]{1,0:T(8,128)S(1)} %reshape.173), kind=kCustom, calls=%fused_computation.6 | custom fusion | flops 24576 | bytes 296448 | tf_op jit(solution)/shard_map/scatter-add | solution.py:67
  154.5 9.4 %minimum_subtract_fusion.2 = (f32[32,256,128]{1,2,0:T(8,128)}, f32[32,256,128]{1,2,0:T(8,128)}) fusion(f32[32,256,128]{1,2,0:T(8,128)} %copy.151, f32[32,256]{1,0:T(8,128)S(1)} %copy-done.1, f32[32,256]{1,0:T(8,128)S(1)} %copy-done.2, bf16[32,256,256]{2,1,0:T(8,128)(2,1)} %param.12, f32[32,256,128]{2,1,0:T(8,128)} %scatter_fusion.1), kind=kOutput, calls=%fused_computation.13 | convolution fusion | flops 541065216 | bytes 21037056 | tf_op jit(solution)/shard_map/fkj,fjs->fks/dot_general | solution.py:70
  163.9 5.6 %copy.156 = f32[32,256,128]{2,1,0:T(8,128)} copy(f32[32,256,128]{1,2,0:T(8,128)} %get-tuple-element.64) | data formatting | bytes 8388608 | tf_op jit(solution)/shard_map/fkj,fjs->fks/dot_general | solution.py:70
  169.5 4.6 gather_fusion.1
  174.5 11.5 %all_to_all.111 = f32[8,6,768]{2,1,0:T(8,128)S(1)} all-to-all(f32[8,6,768]{2,1,0:T(8,128)S(1)} %fusion.40), channel_id=1, replica_groups=mesh['sub'=8,'fdr'=4] {'sub'}, dimensions={0} | all-to-all | bytes 294912 | tf_op jit(solution)/shard_map/all_to_all | solution.py:77
  188.8 3.8 collective-permute-done.3
  193.7 3.4 all-to-all-start.4
  197.1 5.6 %copy.163 = f32[32,256,128]{2,1,0:T(8,128)} copy(f32[32,256,128]{1,2,0:T(8,128)} %get-tuple-element.63) | data formatting | bytes 8388608 | tf_op jit(solution)/shard_map/sub | solution.py:65
  205.2 19.9 %scatter_fusion.2 = f32[32,256,128]{2,1,0:T(8,128)} fusion(f32[32,256,128]{2,1,0:T(8,128)} %copy.163, s32[192]{0:T(256)S(1)} %reshape.165, f32[192,128]{1,0:T(8,128)S(1)} %reshape.179), kind=kCustom, calls=%fused_computation.7 | custom fusion | flops 24576 | bytes 296448 | tf_op jit(solution)/shard_map/scatter-add | solution.py:67
  225.1 9.4 %minimum_subtract_fusion.1 = (f32[32,256,128]{1,2,0:T(8,128)}, f32[32,256,128]{1,2,0:T(8,128)}) fusion(f32[32,256,128]{1,2,0:T(8,128)} %copy.151, f32[32,256]{1,0:T(8,128)S(1)} %copy-done.1, f32[32,256]{1,0:T(8,128)S(1)} %copy-done.2, bf16[32,256,256]{2,1,0:T(8,128)(2,1)} %param.12, f32[32,256,128]{2,1,0:T(8,128)} %scatter_fusion.2), kind=kOutput, calls=%fused_computation.12 | convolution fusion | flops 541065216 | bytes 21037056 | tf_op jit(solution)/shard_map/fkj,fjs->fks/dot_general | solution.py:70
  234.4 5.6 %copy.166 = f32[32,256,128]{2,1,0:T(8,128)} copy(f32[32,256,128]{1,2,0:T(8,128)} %get-tuple-element.67) | data formatting | bytes 8388608 | tf_op jit(solution)/shard_map/fkj,fjs->fks/dot_general | solution.py:70
  240.0 4.6 gather_fusion.2
  245.0 11.5 %all_to_all.112 = f32[8,6,768]{2,1,0:T(8,128)S(1)} all-to-all(f32[8,6,768]{2,1,0:T(8,128)S(1)} %fusion.38), channel_id=1, replica_groups=mesh['sub'=8,'fdr'=4] {'sub'}, dimensions={0} | all-to-all | bytes 294912 | tf_op jit(solution)/shard_map/all_to_all | solution.py:77
  259.2 3.9 collective-permute-done.5
  264.2 3.4 all-to-all-start.6
  267.6 5.6 %copy.173 = f32[32,256,128]{2,1,0:T(8,128)} copy(f32[32,256,128]{1,2,0:T(8,128)} %get-tuple-element.66) | data formatting | bytes 8388608 | tf_op jit(solution)/shard_map/sub | solution.py:65
  275.7 19.9 %scatter_fusion.3 = f32[32,256,128]{2,1,0:T(8,128)} fusion(f32[32,256,128]{2,1,0:T(8,128)} %copy.173, s32[192]{0:T(256)S(1)} %reshape.165, f32[192,128]{1,0:T(8,128)S(1)} %reshape.185), kind=kCustom, calls=%fused_computation.8 | custom fusion | flops 24576 | bytes 296448 | tf_op jit(solution)/shard_map/scatter-add | solution.py:67
  295.6 9.5 %minimum_subtract_fusion = (f32[32,256,128]{1,2,0:T(8,128)}, f32[32,256,128]{1,2,0:T(8,128)}) fusion(f32[32,256,128]{1,2,0:T(8,128)} %copy.151, f32[32,256]{1,0:T(8,128)S(1)} %copy-done.1, f32[32,256]{1,0:T(8,128)S(1)} %copy-done.2, bf16[32,256,256]{2,1,0:T(8,128)(2,1)} %param.12, f32[32,256,128]{2,1,0:T(8,128)} %scatter_fusion.3), kind=kOutput, calls=%fused_computation.11 | convolution fusion | flops 541065216 | bytes 21037056 | tf_op jit(solution)/shard_map/fkj,fjs->fks/dot_general | solution.py:70
  305.2 5.6 %copy.176 = f32[32,256,128]{2,1,0:T(8,128)} copy(f32[32,256,128]{1,2,0:T(8,128)} %get-tuple-element.70) | data formatting | bytes 8388608 | tf_op jit(solution)/shard_map/fkj,fjs->fks/dot_general | solution.py:70
  310.7 4.6 gather_fusion.3
  315.8 11.5 %all_to_all.113 = f32[8,6,768]{2,1,0:T(8,128)S(1)} all-to-all(f32[8,6,768]{2,1,0:T(8,128)S(1)} %fusion.36), channel_id=1, replica_groups=mesh['sub'=8,'fdr'=4] {'sub'}, dimensions={0} | all-to-all | bytes 294912 | tf_op jit(solution)/shard_map/all_to_all | solution.py:77
  329.9 4.0 collective-permute-done.7
  335.0 3.6 all-to-all-start.8
  338.6 5.6 %copy.183 = f32[32,256,128]{2,1,0:T(8,128)} copy(f32[32,256,128]{1,2,0:T(8,128)} %get-tuple-element.69) | data formatting | bytes 8388608 | tf_op jit(solution)/shard_map/sub | solution.py:65
  346.5 19.9 %scatter_fusion.4 = f32[32,256,128]{2,1,0:T(8,128)} fusion(f32[32,256,128]{2,1,0:T(8,128)} %copy.183, s32[192]{0:T(256)S(1)} %reshape.165, f32[192,128]{1,0:T(8,128)S(1)} %reshape.191), kind=kCustom, calls=%fused_computation.9 | custom fusion | flops 24576 | bytes 296448 | tf_op jit(solution)/shard_map/scatter-add | solution.py:67
  366.3 8.4 %minimum_multiply_fusion = (f32[32,256,128]{1,2,0:T(8,128)}, f32[32,256,128]{1,2,0:T(8,128)}) fusion(f32[32]{0:T(128)S(1)} %compare_convert_fusion, f32[32,256]{1,0:T(8,128)S(1)} %copy-done.1, f32[32,256]{1,0:T(8,128)S(1)} %copy-done.2, bf16[32,256,256]{2,1,0:T(8,128)(2,1)} %param.12, f32[32,256,128]{2,1,0:T(8,128)} %scatter_fusion.4), kind=kOutput, calls=%fused_computation.10 | convolution fusion | flops 541065216 | bytes 16842880 | tf_op jit(solution)/shard_map/fkj,fjs->fks/dot_general | solution.py:70
  374.7 5.6 %copy.186 = f32[32,256,128]{2,1,0:T(8,128)} copy(f32[32,256,128]{1,2,0:T(8,128)} %get-tuple-element.72) | data formatting | bytes 8388608 | tf_op jit(solution)/shard_map/fkj,fjs->fks/dot_general | solution.py:70
  380.3 4.6 gather_fusion.4
  385.3 11.5 %all_to_all.114 = f32[8,6,768]{2,1,0:T(8,128)S(1)} all-to-all(f32[8,6,768]{2,1,0:T(8,128)S(1)} %fusion.34), channel_id=1, replica_groups=mesh['sub'=8,'fdr'=4] {'sub'}, dimensions={0} | all-to-all | bytes 294912 | tf_op jit(solution)/shard_map/all_to_all | solution.py:77
  399.3 4.1 collective-permute-done.9
  405.3 3.4 all-to-all-start.10
  408.7 5.6 %copy.197 = f32[32,256,128]{2,1,0:T(8,128)} copy(f32[32,256,128]{1,2,0:T(8,128)} %get-tuple-element.71) | data formatting | bytes 8388608
  419.7 43.3 %all-reduce = (f32[1]{0:T(128)}, f32[1]{0:T(128)}, f32[1]{0:T(128)}, f32[1]{0:T(128)}, f32[1]{0:T(128)}, /*index=5*/f32[1]{0:T(128)}, f32[1]{0:T(128)}, f32[1]{0:T(128)}, f32[1]{0:T(128)}, f32[1]{0:T(128)}) all-reduce(f32[1]{0:T(128)} %bitcast.21, f32[1]{0:T(128)} %bitcast.20, ...), channel_id=1, replica_groups=mesh['sub'=8,'fdr'=4] {'sub','fdr'}, use_global_device_ids=true, to_apply=%region_13.15 | all-reduce | flops 10 | bytes 80 | tf_op jit(solution)/shard_map/psum | solution.py:102
  463.0 2.6 maximum_bitcast_fusion
  467.3 2.5 maximum_bitcast_fusion.2
  (137 shorter events, 40.6 us)
Async XLA Ops:
  0.6 120.4 %copy-start = (f32[32,6,128]{2,0,1:T(8,128)S(1)}, f32[32,6,128]{2,0,1:T(8,128)}, u32[]{:S(2)}) copy-start(f32[32,6,128]{2,0,1:T(8,128)} %param.20) | copy-start | bytes 294916
  2.5 60.7 %all-to-all-start = ((s32[8,6,1]{1,2,0:T(1,128)}), s32[8,6,1]{1,2,0:T(1,128)S(1)}, u32[]{:S(2)}, u32[]{:S(2)}) async-start(s32[8,6,1]{1,2,0:T(1,128)} %bitcast.5), calls=%async_computation | async-start | bytes 8192 | tf_op jit(solution)/shard_map/all_to_all | solution.py:51
  16.7 25.8 %copy-start.1 = (f32[32,256]{1,0:T(8,128)S(1)}, f32[32,256]{1,0:T(8,128)}, u32[]{:S(2)}) copy-start(f32[32,256]{1,0:T(8,128)} %param.14) | copy-start | bytes 98308
  16.7 25.8 %copy-start.2 = (f32[32,256]{1,0:T(8,128)S(1)}, f32[32,256]{1,0:T(8,128)}, u32[]{:S(2)}) copy-start(f32[32,256]{1,0:T(8,128)} %param.15) | copy-start | bytes 98308
  51.9 25.5 %copy-start.5 = (s32[32]{0:T(128)S(1)}, s32[32]{0:T(128)}, u32[]{:S(2)}) copy-start(s32[32]{0:T(128)} %param.17) | copy-start | bytes 388
  51.9 66.6 %copy-start.3 = (f32[32]{0:T(128)S(1)}, f32[32]{0:T(128)}, u32[]{:S(2)}) copy-start(f32[32]{0:T(128)} %param.19) | copy-start | bytes 388
  63.2 13.8 %all-to-all-start.1 = ((f32[8,6,768]{2,1,0:T(8,128)}), f32[8,6,768]{2,1,0:T(8,128)S(1)}, u32[]{:S(2)}, u32[]{:S(2)}) async-start(f32[8,6,768]{2,1,0:T(8,128)} %fusion.42), calls=%async_computation.1 | async-start | bytes 393216 | tf_op jit(solution)/shard_map/all_to_all | solution.py:77
  77.3 38.8 %collective-permute-start = (f32[32,768]{1,0:T(8,128)S(1)}, f32[32,768]{1,0:T(8,128)S(1)}, u32[]{:S(2)}, u32[]{:S(2)}) collective-permute-start(f32[32,768]{1,0:T(8,128)S(1)} %fusion.33), channel_id=1, source_target_pairs={{0,1},{1,0},{2,3},{3,2},{4,5},{5,4},{6,7},{7,6},{8,9},{9,8},{10,11... | collective-permute-start | bytes 294920 | tf_op jit(solution)/shard_map/ppermute | solution.py:85
  116.1 4.9 %collective-permute-start.1 = (f32[32,768]{1,0:T(8,128)S(1)}, f32[32,768]{1,0:T(8,128)S(1)}, u32[]{:S(2)}, u32[]{:S(2)}) collective-permute-start(f32[32,768]{1,0:T(8,128)S(1)} %add.153), channel_id=1, source_target_pairs={{0,2},{1,3},{2,0},{3,1},{4,6},{5,7},{6,4},{7,5},{8,10},{9,11},{10,... | collective-permute-start | bytes 294920 | tf_op jit(solution)/shard_map/ppermute | solution.py:85
  122.1 12.2 %all-to-all-start.2 = ((f32[8,6,768]{2,1,0:T(8,128)}), f32[8,6,768]{2,1,0:T(8,128)S(1)}, u32[]{:S(2)}, u32[]{:S(2)}) async-start(f32[8,6,768]{2,1,0:T(8,128)} %all_to_all.77), calls=%async_computation.2 | async-start | bytes 393216 | tf_op jit(solution)/shard_map/all_to_all | solution.py:95
  186.3 1.4 collective-permute-start.2
  187.7 4.9 %collective-permute-start.3 = (f32[32,768]{1,0:T(8,128)S(1)}, f32[32,768]{1,0:T(8,128)S(1)}, u32[]{:S(2)}, u32[]{:S(2)}) collective-permute-start(f32[32,768]{1,0:T(8,128)S(1)} %add.159), channel_id=1, source_target_pairs={{0,2},{1,3},{2,0},{3,1},{4,6},{5,7},{6,4},{7,5},{8,10},{9,11},{10,... | collective-permute-start | bytes 294920 | tf_op jit(solution)/shard_map/ppermute | solution.py:85
  193.7 11.1 %all-to-all-start.4 = ((f32[8,6,768]{2,1,0:T(8,128)}), f32[8,6,768]{2,1,0:T(8,128)S(1)}, u32[]{:S(2)}, u32[]{:S(2)}) async-start(f32[8,6,768]{2,1,0:T(8,128)} %all_to_all.82), calls=%async_computation.4 | async-start | bytes 393216 | tf_op jit(solution)/shard_map/all_to_all | solution.py:95
  256.9 1.4 collective-permute-start.4
  258.3 4.9 %collective-permute-start.5 = (f32[32,768]{1,0:T(8,128)S(1)}, f32[32,768]{1,0:T(8,128)S(1)}, u32[]{:S(2)}, u32[]{:S(2)}) collective-permute-start(f32[32,768]{1,0:T(8,128)S(1)} %add.164), channel_id=1, source_target_pairs={{0,2},{1,3},{2,0},{3,1},{4,6},{5,7},{6,4},{7,5},{8,10},{9,11},{10,... | collective-permute-start | bytes 294920 | tf_op jit(solution)/shard_map/ppermute | solution.py:85
  264.2 11.1 %all-to-all-start.6 = ((f32[8,6,768]{2,1,0:T(8,128)}), f32[8,6,768]{2,1,0:T(8,128)S(1)}, u32[]{:S(2)}, u32[]{:S(2)}) async-start(f32[8,6,768]{2,1,0:T(8,128)} %all_to_all.87), calls=%async_computation.6 | async-start | bytes 393216 | tf_op jit(solution)/shard_map/all_to_all | solution.py:95
  327.6 1.4 collective-permute-start.6
  329.0 4.9 %collective-permute-start.7 = (f32[32,768]{1,0:T(8,128)S(1)}, f32[32,768]{1,0:T(8,128)S(1)}, u32[]{:S(2)}, u32[]{:S(2)}) collective-permute-start(f32[32,768]{1,0:T(8,128)S(1)} %add.169), channel_id=1, source_target_pairs={{0,2},{1,3},{2,0},{3,1},{4,6},{5,7},{6,4},{7,5},{8,10},{9,11},{10,... | collective-permute-start | bytes 294920 | tf_op jit(solution)/shard_map/ppermute | solution.py:85
  335.0 11.1 %all-to-all-start.8 = ((f32[8,6,768]{2,1,0:T(8,128)}), f32[8,6,768]{2,1,0:T(8,128)S(1)}, u32[]{:S(2)}, u32[]{:S(2)}) async-start(f32[8,6,768]{2,1,0:T(8,128)} %all_to_all.92), calls=%async_computation.8 | async-start | bytes 393216 | tf_op jit(solution)/shard_map/all_to_all | solution.py:95
  397.2 1.4 collective-permute-start.8
  398.5 4.9 %collective-permute-start.9 = (f32[32,768]{1,0:T(8,128)S(1)}, f32[32,768]{1,0:T(8,128)S(1)}, u32[]{:S(2)}, u32[]{:S(2)}) collective-permute-start(f32[32,768]{1,0:T(8,128)S(1)} %add.174), channel_id=1, source_target_pairs={{0,2},{1,3},{2,0},{3,1},{4,6},{5,7},{6,4},{7,5},{8,10},{9,11},{10,... | collective-permute-start | bytes 294920 | tf_op jit(solution)/shard_map/ppermute | solution.py:85
  405.3 12.9 %all-to-all-start.10 = ((f32[8,6,768]{2,1,0:T(8,128)}), f32[8,6,768]{2,1,0:T(8,128)S(1)}, u32[]{:S(2)}, u32[]{:S(2)}) async-start(f32[8,6,768]{2,1,0:T(8,128)} %all_to_all.97), calls=%async_computation.10 | async-start | bytes 393216 | tf_op jit(solution)/shard_map/all_to_all | solution.py:95
  408.7 61.5 %copy-start.4 = (f32[2]{0:T(128)S(1)}, f32[2]{0:T(128)}, u32[]{:S(2)}) copy-start(f32[2]{0:T(128)} %constant.68.clone) | copy-start | bytes 28
